TPU v7x, 32 devices: a whole 2x2x4 slice. The times are simulated.
32 devices in a mesh: grp: 4 (over z), tm: 8 (over y, x, core).
Axes of the slice: x: 2, y: 2, z: 4, core: 2. Of those that a mesh axis runs over, the one named last changes fastest.
Arguments:
- initial: float32 [8, 16384], P('grp'), parts along dimension 0, may hold values from -1 to 1
- forcing: float32 [8, 32, 16384], P('grp', 'tm'), parts along dimension 0, may hold values from -1.8 to 1.8
- fine_blocks: float32 [16, 3, 128, 128], replicated, may hold values from -0.2 to 0.9, as said below
- coarse_blocks: float32 [16, 3, 128, 128], replicated, may hold values from -0.2 to 0.9, as said below
Outputs:
- solution: float32 [8, 32, 16384], P('grp', 'tm'), parts along dimension 0
There are 4 independent parts, one for each index of `grp`. A program takes and returns all parts, laid end to end along the dimension named above; an argument that names none is the same for every part. Nothing has to cross between parts.
Inputs may be any that keep to these rules, and one draw needn't show every extreme that they name: `fine_blocks`: 16 x 3 blocks of 128 x 128. `coarse_blocks`: 16 x 3 blocks of 128 x 128.
All inputs are finite; a program needn't handle non-finite values.
Results may differ from a plain program's by a relative error of at most 0.00013.
Values sent between devices are 32-bit elements; how exact they have to be, the bound alone decides.
A program may use at most 64 MiB of HBM per device.

v0:
```python
import functools

import jax
import jax.numpy as jnp
from jax import lax
from jax.experimental import pallas as pl
from jax.experimental.pallas import tpu as pltpu
from jax.sharding import PartitionSpec as P

M = 4
DELTA = 0.05
MESH = pl.DeviceIdType.MESH


def newton(mixing, delta_t):
    solved = mixing
    for _ in range(2):
        squared = solved * solved
        solved = (mixing + (2.0 * delta_t) * solved * squared) / (
            (1.0 - delta_t) + (3.0 * delta_t) * squared
        )
    return solved


def kernel(
    n, inst, zones, reps,
    init_ref, forc_ref, fine_ref, coarse_ref, out_ref,
    raw, weights, x, ubuf, carr, rbuf, pbuf, qbuf, gbuf,
    load_sem, carr_send, carr_recv, r_send, r_recv,
):
    me = lax.axis_index("tm")
    blk = raw.shape[-1]
    rows = inst * reps
    coarse_dt = DELTA * M

    loads = [pltpu.make_async_copy(ref, raw.at[w], load_sem.at[w]) for w, ref in enumerate((fine_ref, coarse_ref))]
    for load in loads:
        load.start()

    barrier = pltpu.get_barrier_semaphore()
    for step in range(1, n):
        pl.semaphore_signal(barrier, inc=1, device_id={"tm": lax.rem(me + step, n)}, device_id_type=MESH)

    def initial_at(z):
        return jnp.concatenate(
            [init_ref[pl.ds(z * inst + i, reps, stride=zones * inst), :] for i in range(inst)], axis=0
        )

    def forcing_at(slot, z):
        return jnp.concatenate(
            [forc_ref[pl.ds((i * reps * zones + z) * M + slot, reps, stride=zones * M), :] for i in range(inst)],
            axis=0,
        )

    def emit_out(slot, z, value):
        for i in range(inst):
            out_ref[pl.ds((i * reps * zones + z) * M + slot, reps, stride=zones * M), :] = value[
                i * reps : (i + 1) * reps
            ]

    row = lax.broadcasted_iota(jnp.int32, (rows, blk), 0)

    def put(dst, z, value):
        def write(slot, v):
            high = v.astype(jnp.bfloat16)
            low = (v - high.astype(jnp.float32)).astype(jnp.bfloat16)
            x[dst, slot, :rows] = high
            x[dst, slot, rows:] = low

        write(z + 1, value)
        if z == 0:
            rolled = pltpu.roll(value, rows - 1, 0)
            write(zones + 1, jnp.where(row % reps == reps - 1, 0.0, rolled))
        if z == zones - 1:
            rolled = pltpu.roll(value, 1, 0)
            write(0, jnp.where(row % reps == 0, 0.0, rolled))

    def propagate(src, which, delta_t, emit):
        for z in range(zones):
            left = jnp.concatenate([x[src, z + k] for k in range(3)], axis=1)
            acc = jnp.dot(left, weights[which, z], preferred_element_type=jnp.float32)
            mixing = (acc[:rows, :blk] + acc[:rows, blk:]) + (acc[rows:, :blk] + acc[rows:, blk:])
            emit(z, newton(mixing, delta_t))

    def prepare(which):
        loads[which].wait()

        @pl.loop(0, zones)
        def _(z):
            for k in range(3):
                turned = raw[which, z, k].T
                high = turned.astype(jnp.bfloat16)
                weights[which, z, k * blk : (k + 1) * blk, :blk] = high
                weights[which, z, k * blk : (k + 1) * blk, blk:] = (
                    turned - high.astype(jnp.float32)
                ).astype(jnp.bfloat16)

    def fine_steps(first, last, sink):
        def body(t, _):
            p = lax.rem(t, 2)

            def emit(z, s):
                value = s + forcing_at(t, z)
                put(1 - p, z, value)
                sink(t, z, value)

            propagate(p, 0, DELTA, emit)
            return 0

        lax.fori_loop(first, last, body, 0)

    def store_to(buf):
        def emit(z, value):
            buf[z] = value

        return emit

    prepare(0)
    for z in range(zones):
        put(0, z, initial_at(z))
        put(1, z, forcing_at(0, z))
    fine_steps(jnp.where(me == 0, 0, 1), M, lambda t, z, v: store_to(ubuf)(z, v))
    pl.semaphore_wait(barrier, n - 1)

    onward = pltpu.make_async_remote_copy(
        src_ref=ubuf, dst_ref=carr, send_sem=carr_send, recv_sem=carr_recv,
        device_id={"tm": lax.rem(me + 1, n)}, device_id_type=MESH,
    )

    @pl.when(me < n - 1)
    def _():
        onward.start()

    prepare(1)
    for z in range(zones):
        put(0, z, initial_at(z))
    propagate(0, 1, coarse_dt, store_to(pbuf))

    @pl.when(me == 0)
    def _():
        for z in range(zones):
            rbuf[0, z] = ubuf[z] - pbuf[z]

    @pl.when(me > 0)
    def _():
        onward.wait_recv()
        for z in range(zones):
            put(0, z, carr[z])
        propagate(0, 1, coarse_dt, store_to(qbuf))
        fine_steps(0, M, lambda t, z, v: store_to(gbuf)(z, v))
        for z in range(zones):
            rbuf[me, z] = gbuf[z] - qbuf[z]

    def share(step):
        return pltpu.make_async_remote_copy(
            src_ref=rbuf.at[me], dst_ref=rbuf.at[me], send_sem=r_send.at[step], recv_sem=r_recv.at[me],
            device_id={"tm": lax.rem(me + step, n)}, device_id_type=MESH,
        )

    for step in range(n - 1, 0, -1):

        @pl.when(me + step < n)
        def _():
            share(step).start()

    def chain(j, _):
        pltpu.make_async_remote_copy(
            src_ref=rbuf.at[j], dst_ref=rbuf.at[j], send_sem=r_send.at[0], recv_sem=r_recv.at[j],
            device_id={"tm": lax.rem(me + 1, n)}, device_id_type=MESH,
        ).wait_recv()
        for z in range(zones):
            put(0, z, pbuf[z] + rbuf[j, z])
        propagate(0, 1, coarse_dt, store_to(pbuf))
        return 0

    lax.fori_loop(0, me, chain, 0)
    for z in range(zones):
        emit_out(M - 1, z, pbuf[z] + rbuf[me, z])
    fine_steps(0, M - 1, emit_out)

    @pl.when(me < n - 1)
    def _():
        onward.wait_send()

    for step in range(n - 1, 0, -1):

        @pl.when(me + step < n)
        def _():
            share(step).wait_send()


def solution(mesh):
    n = mesh.shape["tm"]

    def body(initial, forcing, fine_blocks, coarse_blocks):
        inst, slots, cells = forcing.shape
        zones, _, blk, _ = fine_blocks.shape
        blocks = cells // blk
        reps = blocks // zones
        rows = inst * reps
        assert slots == M
        init_rows = initial.reshape(inst, blocks, blk).transpose(1, 0, 2).reshape(-1, blk)
        forc_rows = forcing.reshape(inst, slots, blocks, blk).transpose(0, 2, 1, 3).reshape(-1, blk)
        state = pltpu.VMEM((zones, rows, blk), jnp.float32)
        out = pl.pallas_call(
            functools.partial(kernel, n, inst, zones, reps),
            out_shape=jax.ShapeDtypeStruct(forc_rows.shape, jnp.float32),
            in_specs=[pl.BlockSpec(memory_space=pltpu.VMEM)] * 2 + [pl.BlockSpec(memory_space=pl.ANY)] * 2,
            out_specs=pl.BlockSpec(memory_space=pltpu.VMEM),
            scratch_shapes=[
                pltpu.VMEM((2,) + fine_blocks.shape, jnp.float32),
                pltpu.VMEM((2, zones, 3 * blk, 2 * blk), jnp.bfloat16),
                pltpu.VMEM((2, zones + 2, 2 * rows, blk), jnp.bfloat16),
                state,
                state,
                pltpu.VMEM((n, zones, rows, blk), jnp.float32),
                state,
                state,
                state,
                pltpu.SemaphoreType.DMA((2,)),
                pltpu.SemaphoreType.DMA,
                pltpu.SemaphoreType.DMA,
                pltpu.SemaphoreType.DMA((n,)),
                pltpu.SemaphoreType.DMA((n,)),
            ],
            compiler_params=pltpu.CompilerParams(collective_id=0, has_side_effects=True),
        )(init_rows, forc_rows, fine_blocks, coarse_blocks)
        return out.reshape(inst, blocks, slots, blk).transpose(0, 2, 1, 3).reshape(forcing.shape)

    in_specs = (P("grp", None), P("grp", "tm", None), P(), P())
    out_specs = P("grp", "tm", None)
    return jax.shard_map(body, mesh=mesh, in_specs=in_specs, out_specs=out_specs, check_vma=False)
```

profile of v0, /device:TPU:28, one launch (start us, length us, event | category | flops | bytes accessed | tf_op | source)
XLA Modules:
  0.0 51.2 jit_solution(15824620569000052674)
XLA Ops:
  0.0 49.3 %shard_map.46 = f32[1024,128]{1,0:T(8,128)} custom-call(f32[256,128]{1,0:T(8,128)} %bitcast.17, f32[1024,128]{1,0:T(8,128)} %bitcast.16, f32[16,3,128,128]{3,2,1,0:T(8,128)} %fine_ref.1, f32[16,3,128,128]{3,2,1,0:T(8,128)} %coarse_ref.1), custom_call_target="tpu_custom_call" | custom-call | tf_op jit(solution)/shard_map/pallas_call | solution.py:205
  49.3 1.9 %copy.9 = f32[2,4,16384]{2,1,0:T(4,128)} copy(f32[2,4,16384]{2,1,0:T(4,128)} %bitcast.15) | data formatting | bytes 1048576
where the time goes:
time: 51.4 us; the launch traced here: 51.2 us
  Pallas kernels  49.3 us (96%)
  local copies, waits for them, and re-layouts  1.87 us (4%)
    pallas_call x1, Pallas kernels, body(): pl.pallas_call(functools.partial(kernel, n, inst, zones, reps), out_shape...  49.3 us
    unnamed x1, local copies, waits for them, and re-layouts  1.87 us

commit v1 on v0

--- a/solution.py
+++ b/solution.py
@@ -23,19 +23,30 @@
 
 
 def kernel(
-    n, inst, zones, reps,
-    init_ref, forc_ref, fine_ref, coarse_ref, out_ref,
-    raw, weights, x, ubuf, carr, rbuf, pbuf, qbuf, gbuf,
-    load_sem, carr_send, carr_recv, r_send, r_recv,
+    n, inst, zones, reps, pieces,
+    init_hbm, forc_hbm, fine_hbm, coarse_hbm, out_ref,
+    init_ref, forc_ref, raw, weights, x, ubuf, carr, rbuf, pbuf, qbuf,
+    load_sem, state_sem, carr_send, carr_recv, r_send, r_recv, fwd_send,
 ):
     me = lax.axis_index("tm")
     blk = raw.shape[-1]
     rows = inst * reps
     coarse_dt = DELTA * M
-
-    loads = [pltpu.make_async_copy(ref, raw.at[w], load_sem.at[w]) for w, ref in enumerate((fine_ref, coarse_ref))]
-    for load in loads:
-        load.start()
+    part = zones // pieces
+    odd = lax.rem(me, 2)
+
+    def load(which, c):
+        span = pl.ds(c * part, part)
+        return pltpu.make_async_copy((fine_hbm, coarse_hbm)[which].at[span], raw.at[which, span], load_sem.at[which, c])
+
+    state_loads = [
+        pltpu.make_async_copy(init_hbm, init_ref, state_sem.at[0]),
+        pltpu.make_async_copy(forc_hbm, forc_ref, state_sem.at[1]),
+    ]
+    for c in range(pieces):
+        load(0, c).start()
+    for copy in state_loads:
+        copy.start()
 
     barrier = pltpu.get_barrier_semaphore()
     for step in range(1, n):
@@ -83,31 +94,27 @@
             emit(z, newton(mixing, delta_t))
 
     def prepare(which):
-        loads[which].wait()
-
-        @pl.loop(0, zones)
-        def _(z):
-            for k in range(3):
-                turned = raw[which, z, k].T
-                high = turned.astype(jnp.bfloat16)
-                weights[which, z, k * blk : (k + 1) * blk, :blk] = high
-                weights[which, z, k * blk : (k + 1) * blk, blk:] = (
-                    turned - high.astype(jnp.float32)
-                ).astype(jnp.bfloat16)
-
-    def fine_steps(first, last, sink):
-        def body(t, _):
-            p = lax.rem(t, 2)
-
-            def emit(z, s):
-                value = s + forcing_at(t, z)
-                put(1 - p, z, value)
-                sink(t, z, value)
-
-            propagate(p, 0, DELTA, emit)
-            return 0
-
-        lax.fori_loop(first, last, body, 0)
+        @pl.loop(0, pieces)
+        def _(c):
+            load(which, c).wait()
+            for zz in range(part):
+                z = c * part + zz
+                for k in range(3):
+                    turned = raw[which, z, k].T
+                    high = turned.astype(jnp.bfloat16)
+                    weights[which, z, k * blk : (k + 1) * blk, :blk] = high
+                    weights[which, z, k * blk : (k + 1) * blk, blk:] = (
+                        turned - high.astype(jnp.float32)
+                    ).astype(jnp.bfloat16)
+
+    def fine_step(t, src, sink, keep=True):
+        def emit(z, s):
+            value = s + forcing_at(t, z)
+            if keep:
+                put(1 - src, z, value)
+            sink(z, value)
+
+        propagate(src, 0, DELTA, emit)
 
     def store_to(buf):
         def emit(z, value):
@@ -115,11 +122,28 @@
 
         return emit
 
+    def drop(z, value):
+        pass
+
     prepare(0)
-    for z in range(zones):
-        put(0, z, initial_at(z))
-        put(1, z, forcing_at(0, z))
-    fine_steps(jnp.where(me == 0, 0, 1), M, lambda t, z, v: store_to(ubuf)(z, v))
+    for c in range(pieces):
+        load(1, c).start()
+    for copy in state_loads:
+        copy.wait()
+
+    @pl.when(me == 0)
+    def _():
+        for z in range(zones):
+            put(0, z, initial_at(z))
+        fine_step(0, 0, drop)
+
+    @pl.when(me > 0)
+    def _():
+        for z in range(zones):
+            put(1, z, forcing_at(0, z))
+
+    for t in range(1, M):
+        fine_step(t, t % 2, store_to(ubuf) if t == M - 1 else drop, keep=t < M - 1)
     pl.semaphore_wait(barrier, n - 1)
 
     onward = pltpu.make_async_remote_copy(
@@ -147,27 +171,39 @@
         for z in range(zones):
             put(0, z, carr[z])
         propagate(0, 1, coarse_dt, store_to(qbuf))
-        fine_steps(0, M, lambda t, z, v: store_to(gbuf)(z, v))
-        for z in range(zones):
-            rbuf[me, z] = gbuf[z] - qbuf[z]
-
-    def share(step):
+        for t in range(M - 1):
+            fine_step(t, t % 2, drop)
+
+        def right_side(z, value):
+            rbuf[me, z] = value - qbuf[z]
+
+        fine_step(M - 1, (M - 1) % 2, right_side, keep=False)
+
+    def share(target):
         return pltpu.make_async_remote_copy(
-            src_ref=rbuf.at[me], dst_ref=rbuf.at[me], send_sem=r_send.at[step], recv_sem=r_recv.at[me],
-            device_id={"tm": lax.rem(me + step, n)}, device_id_type=MESH,
-        )
-
-    for step in range(n - 1, 0, -1):
-
-        @pl.when(me + step < n)
+            src_ref=rbuf.at[me], dst_ref=rbuf.at[me], send_sem=r_send.at[target], recv_sem=r_recv.at[me],
+            device_id={"tm": target}, device_id_type=MESH,
+        )
+
+    def forward(j):
+        return pltpu.make_async_remote_copy(
+            src_ref=rbuf.at[j], dst_ref=rbuf.at[j], send_sem=fwd_send.at[j], recv_sem=r_recv.at[j],
+            device_id={"tm": lax.rem(me + n - 1, n)}, device_id_type=MESH,
+        )
+
+    for target in range(n - 1, 0, -2):
+
+        @pl.when(me < target)
         def _():
-            share(step).start()
+            share(target).start()
 
     def chain(j, _):
-        pltpu.make_async_remote_copy(
-            src_ref=rbuf.at[j], dst_ref=rbuf.at[j], send_sem=r_send.at[0], recv_sem=r_recv.at[j],
-            device_id={"tm": lax.rem(me + 1, n)}, device_id_type=MESH,
-        ).wait_recv()
+        forward(j).wait_recv()
+
+        @pl.when(jnp.logical_and(odd == 1, j < me - 1))
+        def _():
+            forward(j).start()
+
         for z in range(zones):
             put(0, z, pbuf[z] + rbuf[j, z])
         propagate(0, 1, coarse_dt, store_to(pbuf))
@@ -176,17 +212,24 @@
     lax.fori_loop(0, me, chain, 0)
     for z in range(zones):
         emit_out(M - 1, z, pbuf[z] + rbuf[me, z])
-    fine_steps(0, M - 1, emit_out)
+    for t in range(M - 1):
+        fine_step(t, t % 2, functools.partial(emit_out, t), keep=t < M - 2)
 
     @pl.when(me < n - 1)
     def _():
         onward.wait_send()
 
-    for step in range(n - 1, 0, -1):
-
-        @pl.when(me + step < n)
+    for target in range(n - 1, 0, -2):
+
+        @pl.when(me < target)
         def _():
-            share(step).wait_send()
+            share(target).wait_send()
+
+    def drain(j, _):
+        forward(j).wait_send()
+        return 0
+
+    lax.fori_loop(0, jnp.where(odd == 1, me - 1, 0), drain, 0)
 
 
 def solution(mesh):
@@ -198,16 +241,19 @@
         blocks = cells // blk
         reps = blocks // zones
         rows = inst * reps
-        assert slots == M
+        assert slots == M and n % 2 == 0
+        pieces = 4 if zones % 4 == 0 else 1
         init_rows = initial.reshape(inst, blocks, blk).transpose(1, 0, 2).reshape(-1, blk)
         forc_rows = forcing.reshape(inst, slots, blocks, blk).transpose(0, 2, 1, 3).reshape(-1, blk)
         state = pltpu.VMEM((zones, rows, blk), jnp.float32)
         out = pl.pallas_call(
-            functools.partial(kernel, n, inst, zones, reps),
+            functools.partial(kernel, n, inst, zones, reps, pieces),
             out_shape=jax.ShapeDtypeStruct(forc_rows.shape, jnp.float32),
-            in_specs=[pl.BlockSpec(memory_space=pltpu.VMEM)] * 2 + [pl.BlockSpec(memory_space=pl.ANY)] * 2,
+            in_specs=[pl.BlockSpec(memory_space=pl.ANY)] * 4,
             out_specs=pl.BlockSpec(memory_space=pltpu.VMEM),
             scratch_shapes=[
+                pltpu.VMEM(init_rows.shape, jnp.float32),
+                pltpu.VMEM(forc_rows.shape, jnp.float32),
                 pltpu.VMEM((2,) + fine_blocks.shape, jnp.float32),
                 pltpu.VMEM((2, zones, 3 * blk, 2 * blk), jnp.bfloat16),
                 pltpu.VMEM((2, zones + 2, 2 * rows, blk), jnp.bfloat16),
@@ -216,10 +262,11 @@
                 pltpu.VMEM((n, zones, rows, blk), jnp.float32),
                 state,
                 state,
-                state,
+                pltpu.SemaphoreType.DMA((2, pieces)),
                 pltpu.SemaphoreType.DMA((2,)),
                 pltpu.SemaphoreType.DMA,
                 pltpu.SemaphoreType.DMA,
+                pltpu.SemaphoreType.DMA((n,)),
                 pltpu.SemaphoreType.DMA((n,)),
                 pltpu.SemaphoreType.DMA((n,)),
             ],

time: 51.4 us -> 22.3 us (0.43)
  the two profiles are of different devices: /device:TPU:28 before, /device:TPU:31 now
where the time goes in v1:
time: 22.3 us; the launch traced here: 22.1 us
  Pallas kernels  20.2 us (91%)
  local copies, waits for them, and re-layouts  1.87 us (8%)
    pallas_call x1, Pallas kernels, body(): pl.pallas_call(functools.partial(kernel, n, inst, zones, reps, pieces), o...  20.2 us
    unnamed x1, local copies, waits for them, and re-layouts  1.87 us

profile of v1, /device:TPU:31, one launch (start us, length us, event | category | flops | bytes accessed | tf_op | source)
XLA Modules:
  0.0 22.1 jit_solution(11489181414295875553)
XLA Ops:
  0.0 20.2 %shard_map.46 = f32[1024,128]{1,0:T(8,128)} custom-call(f32[256,128]{1,0:T(8,128)} %bitcast.17, f32[1024,128]{1,0:T(8,128)} %bitcast.16, f32[16,3,128,128]{3,2,1,0:T(8,128)} %fine_hbm.1, f32[16,3,128,128]{3,2,1,0:T(8,128)} %coarse_hbm.1), custom_call_target="tpu_custom_call" | custom-call | tf_op jit(solution)/shard_map/pallas_call | solution.py:249
  20.2 1.9 %copy.9 = f32[2,4,16384]{2,1,0:T(4,128)} copy(f32[2,4,16384]{2,1,0:T(4,128)} %bitcast.15) | data formatting | bytes 1048576

commit v2 on v1

--- a/solution.py
+++ b/solution.py
@@ -97,6 +97,13 @@
         @pl.loop(0, pieces)
         def _(c):
             load(which, c).wait()
+            if which == 0:
+
+                @pl.when(c == pieces - 1)
+                def _():
+                    for later in range(pieces):
+                        load(1, later).start()
+
             for zz in range(part):
                 z = c * part + zz
                 for k in range(3):
@@ -126,8 +133,6 @@
         pass
 
     prepare(0)
-    for c in range(pieces):
-        load(1, c).start()
     for copy in state_loads:
         copy.wait()
 
@@ -248,8 +253,8 @@
         state = pltpu.VMEM((zones, rows, blk), jnp.float32)
         out = pl.pallas_call(
             functools.partial(kernel, n, inst, zones, reps, pieces),
-            out_shape=jax.ShapeDtypeStruct(forc_rows.shape, jnp.float32),
-            in_specs=[pl.BlockSpec(memory_space=pl.ANY)] * 4,
+            out_shape=pltpu.VMEM(forc_rows.shape, jnp.float32),
+            in_specs=[pl.BlockSpec(memory_space=pltpu.HBM)] * 4,
             out_specs=pl.BlockSpec(memory_space=pltpu.VMEM),
             scratch_shapes=[
                 pltpu.VMEM(init_rows.shape, jnp.float32),

time: 22.3 us -> 20.4 us (0.915)
  local copies, waits for them, and re-layouts: 1.87 us -> 0.8 us
  Pallas kernels: 20.2 us -> 19.5 us
    unnamed x1, local copies, waits for them, and re-layouts: 1.87 us -> 0.8 us
    pallas_call x1, Pallas kernels: 20.2 us -> 19.5 us  [body(): pl.pallas_call(functools.partial(kernel, n, inst, zones, reps, pieces), o...]
where the time goes in v2:
time: 20.4 us; the launch traced here: 20.3 us
  Pallas kernels  19.5 us (96%)
  local copies, waits for them, and re-layouts  0.8 us (4%)
    pallas_call x1, Pallas kernels, body(): pl.pallas_call(functools.partial(kernel, n, inst, zones, reps, pieces), o...  19.5 us
    unnamed x1, local copies, waits for them, and re-layouts  0.8 us

profile of v2, /device:TPU:31, one launch (start us, length us, event | category | flops | bytes accessed | tf_op | source)
XLA Modules:
  0.0 20.3 jit_solution(137363473520324477)
XLA Ops:
  0.0 19.5 %shard_map.46 = f32[1024,128]{1,0:T(8,128)S(1)} custom-call(f32[256,128]{1,0:T(8,128)} %bitcast.17, f32[1024,128]{1,0:T(8,128)} %bitcast.16, f32[16,3,128,128]{3,2,1,0:T(8,128)} %fine_hbm.1, f32[16,3,128,128]{3,2,1,0:T(8,128)} %coarse_hbm.1), custom_call_target="tpu_custom_call" | custom-call | tf_op jit(solution)/shard_map/pallas_call | solution.py:254
  19.5 0.8 %copy.9 = f32[2,4,16384]{2,1,0:T(4,128)} copy(f32[2,4,16384]{2,1,0:T(4,128)S(1)} %bitcast.15) | data formatting | bytes 1048576

commit v3 on v2

--- a/solution.py
+++ b/solution.py
@@ -247,7 +247,7 @@
         reps = blocks // zones
         rows = inst * reps
         assert slots == M and n % 2 == 0
-        pieces = 4 if zones % 4 == 0 else 1
+        pieces = 8 if zones % 8 == 0 else 1
         init_rows = initial.reshape(inst, blocks, blk).transpose(1, 0, 2).reshape(-1, blk)
         forc_rows = forcing.reshape(inst, slots, blocks, blk).transpose(0, 2, 1, 3).reshape(-1, blk)
         state = pltpu.VMEM((zones, rows, blk), jnp.float32)

time: 20.4 us -> 21 us (1.029)
  Pallas kernels: 19.5 us -> 20 us
    pallas_call x1, Pallas kernels: 19.5 us -> 20 us  [body(): pl.pallas_call(functools.partial(kernel, n, inst, zones, reps, pieces), o...]
where the time goes in v3:
time: 21 us; the launch traced here: 20.8 us
  Pallas kernels  20 us (95%)
  local copies, waits for them, and re-layouts  0.8 us (4%)
    pallas_call x1, Pallas kernels, body(): pl.pallas_call(functools.partial(kernel, n, inst, zones, reps, pieces), o...  20 us
    unnamed x1, local copies, waits for them, and re-layouts  0.8 us

profile of v3, /device:TPU:31, one launch (start us, length us, event | category | flops | bytes accessed | tf_op | source)
XLA Modules:
  0.0 20.8 jit_solution(10081401500822691704)
XLA Ops:
  0.0 20.0 %shard_map.46 = f32[1024,128]{1,0:T(8,128)S(1)} custom-call(f32[256,128]{1,0:T(8,128)} %bitcast.17, f32[1024,128]{1,0:T(8,128)} %bitcast.16, f32[16,3,128,128]{3,2,1,0:T(8,128)} %fine_hbm.1, f32[16,3,128,128]{3,2,1,0:T(8,128)} %coarse_hbm.1), custom_call_target="tpu_custom_call" | custom-call | tf_op jit(solution)/shard_map/pallas_call | solution.py:254
  20.0 0.8 %copy.9 = f32[2,4,16384]{2,1,0:T(4,128)} copy(f32[2,4,16384]{2,1,0:T(4,128)S(1)} %bitcast.15) | data formatting | bytes 1048576
